TPU v7x, 32 devices: a whole 2x2x4 slice. The times are simulated.
32 devices in a mesh: dp: 8 (over y, x, core), mp: 4 (over z).
Axes of the slice: x: 2, y: 2, z: 4, core: 2. Of those that a mesh axis runs over, the one named last changes fastest.
Arguments:
- tokens: bfloat16 [16384, 1024], P(('dp', 'mp')), may hold values from -6 to 6
- norm_gain: float32 [2, 1024], replicated, may hold values from 0.1 to 1.9
- qkv_weight: bfloat16 [3, 1024, 1024], P(None, 'dp', 'mp')
- out_weight: bfloat16 [1024, 1024], P('mp', 'dp'), may hold values from -0.1875 to 0.1875
- variate_bias: float32 [2, 16], replicated, may hold values from -6 to 6
- ffn_weight: bfloat16 [2, 1024, 2816], P(None, 'dp', 'mp'), may hold values from -0.1875 to 0.1875
- down_weight: bfloat16 [2816, 1024], P('mp', 'dp'), may hold values from -0.109375 to 0.109375
- sample_ids: int32 [16384], P(('dp', 'mp')), may hold values from 0 to 127, as said below
- variate_ids: int32 [16384], P(('dp', 'mp')), may hold values from 0 to 15, as said below
- time_ids: int32 [16384], P(('dp', 'mp')), may hold values from 0 to 31, as said below
Outputs:
- encoded: bfloat16 [16384, 1024], P(('dp', 'mp'))
Inputs may be any that keep to these rules, and one draw needn't show every extreme that they name: `sample_ids`: within each packed sequence of 512 tokens the series numbers start at 0 and never fall; a series with v variates (1 to 16) and p patches (4 to 32) holds v * p consecutive tokens, the last series of a sequence may be cut short; some packed sequence holds 128 series of one variate and four patches each. `variate_ids`: A token's offset within its series divided by that series' patch count p. `time_ids`: A token's offset within its series modulo that series' patch count p.
All inputs are finite; a program needn't handle non-finite values.
Results may differ from a plain program's by a relative error of at most 0.017.
Values may be sent and summed in bfloat16 or wider, within the bound.
A program may use at most 128 MiB of HBM per device.

v0:
```python
import jax
import jax.numpy as jnp
from jax import lax
from jax.sharding import PartitionSpec as P

HEAD_DIM = 64
L = 512


def rms_norm(values, gain):
    wide = values.astype(jnp.float32)
    square = jnp.mean(wide * wide, axis=-1, keepdims=True)
    return (wide * lax.rsqrt(square + 1e-05) * gain[None, :]).astype(jnp.bfloat16)


def rotate(values, times):
    half = values.shape[-1] // 2
    freq = 10000.0 ** (-jnp.arange(half, dtype=jnp.float32) / half)
    angle = times.astype(jnp.float32)[:, None] * freq[None, :]
    cosine = jnp.cos(angle)[:, None, :]
    sine = jnp.sin(angle)[:, None, :]
    first = values[..., :half]
    second = values[..., half:]
    return jnp.concatenate(
        [first * cosine - second * sine, first * sine + second * cosine], axis=-1
    )


def rotated(raw, times):
    row_total, local_width = raw.shape
    turned = rotate(raw.reshape(row_total, local_width // HEAD_DIM, HEAD_DIM), times)
    return turned.reshape(row_total, local_width).astype(jnp.bfloat16)


def attend(queries, keys_rot, values, samples, variates, bias):
    row_total, local_width = queries.shape
    heads_here = local_width // HEAD_DIM
    count = row_total // L

    def one_sequence(args):
        qs, ks, vs, sample_row, variate_row = args
        scores = jnp.einsum(
            "qhd,khd->hqk", qs, ks, preferred_element_type=jnp.float32
        ) * HEAD_DIM ** (-0.5)
        same = variate_row[:, None] == variate_row[None, :]
        scores = scores + jnp.where(same[None], bias[0][:, None, None], bias[1][:, None, None])
        scores = jnp.where((sample_row[:, None] == sample_row[None, :])[None], scores, -1e30)
        top = jnp.max(scores, axis=2, keepdims=True)
        expo = jnp.exp(scores - top)
        weights = (expo / jnp.sum(expo, axis=2, keepdims=True)).astype(jnp.bfloat16)
        return jnp.einsum("hqk,khd->qhd", weights, vs, preferred_element_type=jnp.float32).astype(
            jnp.bfloat16
        )

    shape = (count, L, heads_here, HEAD_DIM)
    result = lax.map(
        one_sequence,
        (
            queries.reshape(shape),
            keys_rot.reshape(shape),
            values.reshape(shape),
            samples.reshape(count, L),
            variates.reshape(count, L),
        ),
    )
    return result.reshape(row_total, local_width)


def local(
    tokens,
    norm_gain,
    qkv_weight,
    out_weight,
    variate_bias,
    ffn_weight,
    down_weight,
    sample_ids,
    variate_ids,
    time_ids,
):
    heads_here = qkv_weight.shape[2] // HEAD_DIM
    head_start = lax.axis_index("mp") * heads_here
    bias_local = lax.dynamic_slice_in_dim(variate_bias, head_start, heads_here, 1)
    first_normed = rms_norm(tokens, norm_gain[0])
    wide_columns = lax.all_gather(qkv_weight, "mp", axis=2, tiled=True)
    columns = first_normed
    projected = jnp.einsum(
        "rc,jcd->jrd",
        columns,
        lax.all_gather(wide_columns, "dp", axis=1, tiled=True),
        preferred_element_type=jnp.float32,
    )
    queries = rotated(projected[0], time_ids)
    keys_rot = rotated(projected[1], time_ids)
    values = projected[2].astype(jnp.bfloat16)
    grouped = lax.all_to_all(
        jnp.stack([queries, keys_rot, values]), "mp", split_axis=2, concat_axis=1, tiled=True
    )
    gathered_ids = (
        lax.all_gather(sample_ids, "mp", axis=0, tiled=True),
        lax.all_gather(variate_ids, "mp", axis=0, tiled=True),
    )
    attended = attend(
        grouped[0], grouped[1], grouped[2], gathered_ids[0], gathered_ids[1], bias_local
    )
    back_rows = lax.all_to_all(attended, "mp", split_axis=0, concat_axis=1, tiled=True)
    out_rows = lax.all_gather(out_weight, "mp", axis=0, tiled=True)
    mixed = jnp.dot(
        back_rows,
        lax.all_gather(out_rows, "dp", axis=1, tiled=True),
        preferred_element_type=jnp.float32,
    )
    residual = (tokens.astype(jnp.float32) + mixed).astype(jnp.bfloat16)
    second_normed = rms_norm(residual, norm_gain[1])
    ffn_columns = lax.all_gather(ffn_weight, "mp", axis=2, tiled=True)
    columns = second_normed
    gate_up = jnp.einsum(
        "rc,jcf->jrf",
        columns,
        lax.all_gather(ffn_columns, "dp", axis=1, tiled=True),
        preferred_element_type=jnp.float32,
    )
    hidden = (jax.nn.silu(gate_up[0]) * gate_up[1]).astype(jnp.bfloat16)
    down_full = lax.all_gather(down_weight, "mp", axis=0, tiled=True)
    feed = jnp.dot(
        hidden,
        lax.all_gather(down_full, "dp", axis=1, tiled=True),
        preferred_element_type=jnp.float32,
    )
    return (residual.astype(jnp.float32) + feed).astype(jnp.bfloat16)


def solution(mesh):
    return jax.shard_map(
        local,
        mesh=mesh,
        in_specs=(
            P(("dp", "mp"), None),
            P(),
            P(None, "dp", "mp"),
            P("mp", "dp"),
            P(),
            P(None, "dp", "mp"),
            P("mp", "dp"),
            P(("dp", "mp")),
            P(("dp", "mp")),
            P(("dp", "mp")),
        ),
        out_specs=P(("dp", "mp"), None),
        check_vma=False,
    )
```

profile of v0, /device:TPU:0, one launch (start us, length us, event | category | flops | bytes accessed | tf_op | source)
XLA Modules:
  0.0 358.3 jit_solution(14907393396261247635)
XLA Ops:
  6.5 2.2 copy.40
  8.8 27.7 %all_gather.30 = bf16[3,128,1024]{2,1,0:T(8,128)(2,1)} all-gather(bf16[3,128,256]{2,1,0:T(8,128)(2,1)} %param.14), channel_id=1, replica_groups=mesh['dp'=8,'mp'=4] {'mp'}, dimensions={2}, use_global_device_ids=true | all-gather | bytes 983040 | tf_op jit(solution)/shard_map/all_gather | solution.py:85
  36.6 18.9 %all_gather.34 = bf16[1024,128]{1,0:T(8,128)(2,1)} all-gather(bf16[256,128]{1,0:T(8,128)(2,1)} %param.15), channel_id=1, replica_groups=mesh['dp'=8,'mp'=4] {'mp'}, dimensions={0}, use_global_device_ids=true | all-gather | bytes 327680 | tf_op jit(solution)/shard_map/all_gather | solution.py:107
  55.5 1.2 all-gather.12.cloned.1.call-done
  56.8 4.9 %copy.41 = bf16[2,128,2816]{2,1,0:T(8,128)(2,1)} copy(bf16[2,128,2816]{1,0,2:T(2,128)(2,1)} %all-gather.12.cloned.1.call-done) | data formatting | bytes 2883584 | tf_op jit(solution)/shard_map/all_gather | solution.py:115
  61.7 0.3 fusion.56
  62.0 0.3 multiply_cosine_fusion
  62.3 41.2 %all-gather.8.cloned.1.call-done = bf16[3,1024,1024]{2,1,0:T(8,128)(2,1)} async-done(((bf16[3,128,1024]{2,1,0:T(8,128)(2,1)}), bf16[3,1024,1024]{2,1,0:T(8,128)(2,1)}) %all-gather.8.cloned.1.call-update) | async-done | bytes 6291472 | tf_op jit(solution)/shard_map/all_gather | solution.py:90
  103.5 5.7 %convolution_bitcast_fusion.1 = f32[3,512,1024]{2,1,0:T(8,128)S(1)} fusion(bf16[3,1024,1024]{2,1,0:T(8,128)(2,1)} %all-gather.8.cloned.1.call-done, bf16[512,1024]{1,0:T(8,128)(2,1)S(1)} %copy-done.2, f32[1024]{0:T(1024)S(1)} %bitcast.128, f32[512]{0:T(512)S(1)} %add_rsqrt_fusion.1), kind=kOutput, calls=%fused_computation.54 | convolution fusion | flops 3223322624 | bytes 13637632 | tf_op jit(solution)/shard_map/rc,jcd->jrd/dot_general | solution.py:87
  109.3 1.1 slice.103
  110.4 2.4 fusion.80
  112.8 2.0 copy.34
  114.8 2.9 copy.35
  117.7 2.3 subtract_convert_fusion.1
  120.0 0.1 pad_maximum_fusion.1
  120.1 1.3 copy.36
  121.5 1.3 copy.37
  122.8 2.5 pad_maximum_fusion
  125.3 5.7 %copy.38 = bf16[3,512,1024]{1,0,2:T(4,128)(2,1)} copy(bf16[3,512,1024]{2,1,0:T(8,128)(2,1)S(1)} %pad_maximum_fusion) | data formatting | bytes 6291456 | tf_op jit(solution)/shard_map/stack | solution.py:97
  131.0 5.0 %all-to-all-start = ((bf16[3,512,1024]{1,0,2:T(4,128)(2,1)}), bf16[3,512,1024]{1,0,2:T(4,128)(2,1)}, u32[]{:S(2)}, u32[]{:S(2)}) async-start(bf16[3,512,1024]{1,0,2:T(4,128)(2,1)} %copy.38), calls=%async_computation | async-start | bytes 8388608 | tf_op jit(solution)/shard_map/all_to_all | solution.py:96
  136.1 106.7 %all_gather.38 = bf16[2816,128]{1,0:T(8,128)(2,1)} all-gather(bf16[704,128]{1,0:T(8,128)(2,1)S(1)} %copy-done.4), channel_id=1, replica_groups=mesh['dp'=8,'mp'=4] {'mp'}, dimensions={0}, use_global_device_ids=true | all-gather | bytes 901120 | tf_op jit(solution)/shard_map/all_gather | solution.py:124
  242.9 11.9 %all-gather.1 = s32[4,1,512]{2,1,0:T(1,128)S(1)} all-gather(s32[1,1,512]{2,1,0:T(1,128)S(1)} %bitcast.129), channel_id=1, replica_groups=mesh['dp'=8,'mp'=4] {'mp'}, dimensions={0}, use_global_device_ids=true | all-gather | bytes 10240 | tf_op jit(solution)/shard_map/all_gather | solution.py:101
  254.8 12.1 %all-gather = s32[4,1,512]{2,1,0:T(1,128)S(1)} all-gather(s32[1,1,512]{2,1,0:T(1,128)S(1)} %bitcast.130), channel_id=1, replica_groups=mesh['dp'=8,'mp'=4] {'mp'}, dimensions={0}, use_global_device_ids=true | all-gather | bytes 10240 | tf_op jit(solution)/shard_map/all_gather | solution.py:100
  266.9 0.1 constant_dynamic-slice_fusion.2
  267.0 3.2 copy.39
  270.2 1.5 fusion.81
  271.7 31.2 %while.10 = (s32[]{:T(128)}, bf16[4,512,4,64]{1,3,2,0:T(8,128)(2,1)}, bf16[4,512,4,64]{1,3,2,0:T(8,128)(2,1)}, s32[4,512]{1,0:T(4,128)S(1)}, bf16[4,512,4,64]{1,...) while((s32[]{:T(128)}, ...), condition=%wide.region_4.5_spmd, body=%wide.region_1.4_spmd.sunk | while | flops 416943104 | bytes 3179681 | solution.py:56
  271.7 0.2 broadcast_compare_fusion.4
  271.9 0.2 broadcast_compare_fusion.5
  272.2 3.0 fusion.100
  275.2 4.3 %fusion.101 = bf16[4,512,4,64]{1,3,2,0:T(8,128)(2,1)} fusion(bf16[4,512,4,64]{1,3,2,0:T(8,128)(2,1)} %get-tuple-element.154, s32[]{:T(128)} %get-tuple-element.153, f32[4,512]{1,0:T(4,128)S(1)} %fusion.100, bf16[4,512,4,64]{1,3,2,0:T(8,128)(2,1)} %get-tuple-element.164, f32[4]{0:T(128)S(1)} %get-tuple-element.140, f32[4]{0:T(128)S(1)} %get-tuple-element.141, ...), kind=kOutput, calls=%fused_computation.14.clone.1 | convolution fusion | flops 275909120 | bytes 1584128 | tf_op jit(solution)/shard_map/while/body/eval_jaxpr/hqk,khd->qhd/dot_general | solution.py:51
  279.5 0.2 broadcast_compare_fusion.4
  279.7 0.2 broadcast_compare_fusion.5
  280.0 3.0 fusion.100
  283.0 4.3 %fusion.101 = bf16[4,512,4,64]{1,3,2,0:T(8,128)(2,1)} fusion(bf16[4,512,4,64]{1,3,2,0:T(8,128)(2,1)} %get-tuple-element.154, s32[]{:T(128)} %get-tuple-element.153, f32[4,512]{1,0:T(4,128)S(1)} %fusion.100, bf16[4,512,4,64]{1,3,2,0:T(8,128)(2,1)} %get-tuple-element.164, f32[4]{0:T(128)S(1)} %get-tuple-element.140, f32[4]{0:T(128)S(1)} %get-tuple-element.141, ...), kind=kOutput, calls=%fused_computation.14.clone.1 | convolution fusion | flops 275909120 | bytes 1584128 | tf_op jit(solution)/shard_map/while/body/eval_jaxpr/hqk,khd->qhd/dot_general | solution.py:51
  287.3 0.2 broadcast_compare_fusion.4
  287.5 0.2 broadcast_compare_fusion.5
  287.8 3.0 fusion.100
  290.8 4.3 %fusion.101 = bf16[4,512,4,64]{1,3,2,0:T(8,128)(2,1)} fusion(bf16[4,512,4,64]{1,3,2,0:T(8,128)(2,1)} %get-tuple-element.154, s32[]{:T(128)} %get-tuple-element.153, f32[4,512]{1,0:T(4,128)S(1)} %fusion.100, bf16[4,512,4,64]{1,3,2,0:T(8,128)(2,1)} %get-tuple-element.164, f32[4]{0:T(128)S(1)} %get-tuple-element.140, f32[4]{0:T(128)S(1)} %get-tuple-element.141, ...), kind=kOutput, calls=%fused_computation.14.clone.1 | convolution fusion | flops 275909120 | bytes 1584128 | tf_op jit(solution)/shard_map/while/body/eval_jaxpr/hqk,khd->qhd/dot_general | solution.py:51
  295.1 0.2 broadcast_compare_fusion.4
  295.4 0.2 broadcast_compare_fusion.5
  295.6 3.0 fusion.100
  298.6 4.3 %fusion.101 = bf16[4,512,4,64]{1,3,2,0:T(8,128)(2,1)} fusion(bf16[4,512,4,64]{1,3,2,0:T(8,128)(2,1)} %get-tuple-element.154, s32[]{:T(128)} %get-tuple-element.153, f32[4,512]{1,0:T(4,128)S(1)} %fusion.100, bf16[4,512,4,64]{1,3,2,0:T(8,128)(2,1)} %get-tuple-element.164, f32[4]{0:T(128)S(1)} %get-tuple-element.140, f32[4]{0:T(128)S(1)} %get-tuple-element.141, ...), kind=kOutput, calls=%fused_computation.14.clone.1 | convolution fusion | flops 275909120 | bytes 1584128 | tf_op jit(solution)/shard_map/while/body/eval_jaxpr/hqk,khd->qhd/dot_general | solution.py:51
  302.9 3.7 %all-to-all-start.1 = ((bf16[4,512,256]{1,2,0:T(8,128)(2,1)}), bf16[4,512,256]{1,2,0:T(8,128)(2,1)S(1)}, u32[]{:S(2)}, u32[]{:S(2)}) async-start(bf16[4,512,256]{1,2,0:T(8,128)(2,1)} %bitcast.24), calls=%async_computation.1 | async-start | bytes 2097152 | tf_op jit(solution)/shard_map/all_to_all | solution.py:106
  306.7 18.6 %all-to-all-done.1 = bf16[4,512,256]{1,2,0:T(8,128)(2,1)S(1)} async-done(((bf16[4,512,256]{1,2,0:T(8,128)(2,1)}), bf16[4,512,256]{1,2,0:T(8,128)(2,1)S(1)}, u32[]{:S(2)}, u32[]{:S(2)}) %all-to-all-start.1) | async-done | bytes 1048608 | tf_op jit(solution)/shard_map/all_to_all | solution.py:106
  325.3 3.0 fusion.60
  328.3 13.2 %convolution_bitcast_fusion = f32[2,512,2816]{2,1,0:T(8,128)} fusion(bf16[2,1024,2816]{2,1,0:T(8,128)(2,1)} %all-gather.14.cloned.1.call-done, bf16[512,1024]{1,0:T(8,128)(2,1)S(1)} %get-tuple-element.84, f32[1024]{0:T(1024)S(1)} %bitcast.125, f32[512]{0:T(512)S(1)} %add_rsqrt_fusion), kind=kOutput, calls=%fused_computation.41 | convolution fusion | flops 5907677184 | bytes 24123392 | tf_op jit(solution)/shard_map/rc,jcf->jrf/dot_general | solution.py:117
  341.6 10.2 %fusion.63 = bf16[512,1024]{1,0:T(8,128)(2,1)} fusion(bf16[512,1024]{1,0:T(8,128)(2,1)S(1)} %get-tuple-element.84, bf16[2816,1024]{1,0:T(8,128)(2,1)} %all-gather.16.cloned.1.call-done, f32[2,512,2816]{2,1,0:T(8,128)} %convolution_bitcast_fusion), kind=kOutput, calls=%fused_computation.62 | convolution fusion | flops 2963013632 | bytes 19398656 | tf_op jit(solution)/shard_map/dot_general | solution.py:125
  (48 shorter events, 0.4 us)
Async XLA Ops:
  6.5 260.4 %copy-start = (f32[2,16]{1,0:T(2,128)S(1)}, f32[2,16]{1,0:T(2,128)}, u32[]{:S(2)}) copy-start(f32[2,16]{1,0:T(2,128)} %param.16) | copy-start | bytes 388
  6.5 55.1 %copy-start.8 = (s32[512]{0:T(512)S(1)}, s32[512]{0:T(512)}, u32[]{:S(2)}) copy-start(s32[512]{0:T(512)} %param.21) | copy-start | bytes 6148
  6.5 55.2 %copy-start.2 = (bf16[512,1024]{1,0:T(8,128)(2,1)S(1)}, bf16[512,1024]{1,0:T(8,128)(2,1)}, u32[]{:S(2)}) copy-start(bf16[512,1024]{1,0:T(8,128)(2,1)} %param.12) | copy-start | bytes 3145732
  6.5 50.2 %all-gather.12.cloned.1.call-start = ((), (), s32[]{:S(2)}) async-start(), calls=%async_computation.4 | async-start | bytes 1802240 | tf_op jit(solution)/shard_map/all_gather | solution.py:115
  8.7 53.3 %copy-start.5 = (f32[2,1024]{1,0:T(2,128)S(1)}, f32[2,1024]{1,0:T(2,128)}, u32[]{:S(2)}) copy-start(f32[2,1024]{1,0:T(2,128)} %param.13) | copy-start | bytes 24580
  8.8 94.8 %all-gather.8.cloned.1.call-start = ((), (), s32[]{:S(2)}) async-start(), calls=%async_computation.2 | async-start | bytes 7077888 | tf_op jit(solution)/shard_map/all_gather | solution.py:90
  36.5 270.2 %all-gather.10.cloned.1.call-start = ((), (), s32[]{:S(2)}) async-start(), calls=%async_computation.3 | async-start | bytes 2359296 | tf_op jit(solution)/shard_map/all_gather | solution.py:110
  55.5 272.8 %all-gather.14.cloned.1.call-start = ((), (), s32[]{:S(2)}) async-start(), calls=%async_computation.5 | async-start | bytes 12976128 | tf_op jit(solution)/shard_map/all_gather | solution.py:120
  131.0 5.1 %copy-start.4 = (bf16[704,128]{1,0:T(8,128)(2,1)S(1)}, bf16[704,128]{1,0:T(8,128)(2,1)}, u32[]{:S(2)}) copy-start(bf16[704,128]{1,0:T(8,128)(2,1)} %param.18) | copy-start | bytes 540676
  131.0 111.8 %copy-start.6 = (s32[512]{0:T(512)S(1)}, s32[512]{0:T(512)}, u32[]{:S(2)}) copy-start(s32[512]{0:T(512)} %param.20) | copy-start | bytes 6148
  131.0 123.8 %copy-start.7 = (s32[512]{0:T(512)S(1)}, s32[512]{0:T(512)}, u32[]{:S(2)}) copy-start(s32[512]{0:T(512)} %param.19) | copy-start | bytes 6148
  131.0 136.0 %all-to-all-start = ((bf16[3,512,1024]{1,0,2:T(4,128)(2,1)}), bf16[3,512,1024]{1,0,2:T(4,128)(2,1)}, u32[]{:S(2)}, u32[]{:S(2)}) async-start(bf16[3,512,1024]{1,0,2:T(4,128)(2,1)} %copy.38), calls=%async_computation | async-start | bytes 8388608 | tf_op jit(solution)/shard_map/all_to_all | solution.py:96
  136.0 205.6 %all-gather.16.cloned.1.call-start = ((), (), s32[]{:S(2)}) async-start(), calls=%async_computation.6 | async-start | bytes 6488064 | tf_op jit(solution)/shard_map/all_gather | solution.py:127
  271.7 53.6 %copy-start.3 = (bf16[512,1024]{1,0:T(8,128)(2,1)S(1)}, bf16[512,1024]{1,0:T(8,128)(2,1)}, u32[]{:S(2)}) copy-start(bf16[512,1024]{1,0:T(8,128)(2,1)} %param.12) | copy-start | bytes 3145732
  302.9 22.3 %all-to-all-start.1 = ((bf16[4,512,256]{1,2,0:T(8,128)(2,1)}), bf16[4,512,256]{1,2,0:T(8,128)(2,1)S(1)}, u32[]{:S(2)}, u32[]{:S(2)}) async-start(bf16[4,512,256]{1,2,0:T(8,128)(2,1)} %bitcast.24), calls=%async_computation.1 | async-start | bytes 2097152 | tf_op jit(solution)/shard_map/all_to_all | solution.py:106
  341.6 10.2 %copy-start.1 = (f32[2,16]{1,0:T(2,128)S(1)}, f32[2,16]{1,0:T(2,128)}, u32[]{:S(2)}) copy-start(f32[2,16]{1,0:T(2,128)} %param.16) | copy-start | bytes 388
Sparse Core Ops, SparseCore 0:
  8.9 47.8 all-gather.11
  58.7 44.7 all-gather.7
  105.4 28.0 all-gather.9
  135.3 67.5 all-gather.13
  243.0 44.4 all-gather.15
where the time goes:
time: 359 us; the launch traced here: 358 us
  blocking collectives  177 us (49%)
  matrix products  61.5 us (17%)
  waiting for transfers between devices  61.1 us (17%)
  local copies, waits for them, and re-layouts  28.7 us (8%)
  between operations  13.3 us (4%)
  starting transfers between devices  8.9 us (2%)
  other arithmetic  7.24 us (2%)
    all_gather x1, blocking collectives, local(): down_full = lax.all_gather(down_weight, 'mp', axis=0, tiled=True)  107 us
    all_gather x1, waiting for transfers between devices, local(): lax.all_gather(wide_columns, 'dp', axis=1, tiled=True)  41.2 us
    all_gather x1, blocking collectives, local(): wide_columns = lax.all_gather(qkv_weight, 'mp', axis=2, tiled=True)  27.7 us
    all_gather x1, blocking collectives, local(): out_rows = lax.all_gather(out_weight, 'mp', axis=0, tiled=True)  18.9 us
    all_to_all x1, waiting for transfers between devices, local(): lax.all_to_all(attended, 'mp', split_axis=0, concat_axis=1, tiled=True)  18.6 us
    dot_general x4, matrix products, one_sequence(): jnp.einsum('hqk,khd->qhd', weights, vs, preferred_element_type=jnp.float32)  17.2 us
    dot_general x1, matrix products, local(): jnp.einsum('rc,jcf->jrf', columns, lax.all_gather(ffn_columns, 'dp', axis...  13.2 us
    sub x4, matrix products, one_sequence(): expo = jnp.exp(scores - top)  12.1 us
  transfers between devices with their start and end apart: 7, of which 3 were waited for; matrix products, arithmetic and copies ran while one was open for 24% of the time, Pallas kernels for 0%

commit v1 on v0

--- a/solution.py
+++ b/solution.py
@@ -107,7 +107,7 @@
     out_rows = lax.all_gather(out_weight, "mp", axis=0, tiled=True)
     mixed = jnp.dot(
         back_rows,
-        lax.all_gather(out_rows, "dp", axis=1, tiled=True),
+        jnp.concatenate(lax.all_gather(out_rows, "dp"), axis=1),
         preferred_element_type=jnp.float32,
     )
     residual = (tokens.astype(jnp.float32) + mixed).astype(jnp.bfloat16)

time: 359 us -> 356 us (level)
  matrix products: 61.5 us -> 57.4 us
    sub x4, matrix products: 12.1 us -> 8.39 us  [one_sequence(): expo = jnp.exp(scores - top)]
where the time goes in v1:
time: 356 us; the launch traced here: 355 us
  blocking collectives  177 us (50%)
  waiting for transfers between devices  58.3 us (16%)
  matrix products  57.4 us (16%)
  local copies, waits for them, and re-layouts  32.2 us (9%)
  between operations  13.3 us (4%)
  starting transfers between devices  8.9 us (2%)
  other arithmetic  7.3 us (2%)
    all_gather x1, blocking collectives, local(): down_full = lax.all_gather(down_weight, 'mp', axis=0, tiled=True)  107 us
    all_gather x1, waiting for transfers between devices, local(): lax.all_gather(wide_columns, 'dp', axis=1, tiled=True)  41.2 us
    all_gather x1, blocking collectives, local(): wide_columns = lax.all_gather(qkv_weight, 'mp', axis=2, tiled=True)  27.7 us
    all_gather x1, blocking collectives, local(): out_rows = lax.all_gather(out_weight, 'mp', axis=0, tiled=True)  18.9 us
    dot_general x4, matrix products, one_sequence(): jnp.einsum('hqk,khd->qhd', weights, vs, preferred_element_type=jnp.float32)  16.9 us
    all_to_all x1, waiting for transfers between devices, local(): lax.all_to_all(attended, 'mp', split_axis=0, concat_axis=1, tiled=True)  15.7 us
    dot_general x1, matrix products, local(): jnp.einsum('rc,jcf->jrf', columns, lax.all_gather(ffn_columns, 'dp', axis...  13.2 us
    all_gather x1, blocking collectives, local(): lax.all_gather(sample_ids, 'mp', axis=0, tiled=True)  12.1 us
  transfers between devices with their start and end apart: 7, of which 3 were waited for; matrix products, arithmetic and copies ran while one was open for 24% of the time, Pallas kernels for 0%

profile of v1, /device:TPU:0, one launch (start us, length us, event | category | flops | bytes accessed | tf_op | source)
XLA Modules:
  0.0 354.9 jit_solution(12842004485942888871)
XLA Ops:
  6.5 2.2 copy.52
  8.8 27.7 %all_gather.33 = bf16[3,128,1024]{2,1,0:T(8,128)(2,1)} all-gather(bf16[3,128,256]{2,1,0:T(8,128)(2,1)} %param.14), channel_id=1, replica_groups=mesh['dp'=8,'mp'=4] {'mp'}, dimensions={2}, use_global_device_ids=true | all-gather | bytes 983040 | tf_op jit(solution)/shard_map/all_gather | solution.py:85
  36.6 18.9 %all_gather.37 = bf16[1024,128]{1,0:T(8,128)(2,1)} all-gather(bf16[256,128]{1,0:T(8,128)(2,1)} %param.15), channel_id=1, replica_groups=mesh['dp'=8,'mp'=4] {'mp'}, dimensions={0}, use_global_device_ids=true | all-gather | bytes 327680 | tf_op jit(solution)/shard_map/all_gather | solution.py:107
  55.5 1.2 all-gather.11.cloned.1.call-done
  56.8 4.9 %copy.53 = bf16[2,128,2816]{2,1,0:T(8,128)(2,1)} copy(bf16[2,128,2816]{1,0,2:T(2,128)(2,1)} %all-gather.11.cloned.1.call-done) | data formatting | bytes 2883584 | tf_op jit(solution)/shard_map/all_gather | solution.py:115
  61.7 0.3 fusion.56
  62.0 0.3 multiply_cosine_fusion
  62.3 41.2 %all-gather.9.cloned.1.call-done = bf16[3,1024,1024]{2,1,0:T(8,128)(2,1)} async-done(((bf16[3,128,1024]{2,1,0:T(8,128)(2,1)}), bf16[3,1024,1024]{2,1,0:T(8,128)(2,1)}) %all-gather.9.cloned.1.call-update) | async-done | bytes 6291472 | tf_op jit(solution)/shard_map/all_gather | solution.py:90
  103.5 5.7 %convolution_bitcast_fusion.1 = f32[3,512,1024]{2,1,0:T(8,128)S(1)} fusion(bf16[3,1024,1024]{2,1,0:T(8,128)(2,1)} %all-gather.9.cloned.1.call-done, bf16[512,1024]{1,0:T(8,128)(2,1)S(1)} %copy-done.2, f32[1024]{0:T(1024)S(1)} %bitcast.134, f32[512]{0:T(512)S(1)} %add_rsqrt_fusion.1), kind=kOutput, calls=%fused_computation.54 | convolution fusion | flops 3223322624 | bytes 13637632 | tf_op jit(solution)/shard_map/rc,jcd->jrd/dot_general | solution.py:87
  109.3 1.1 slice.103
  110.4 2.4 fusion.80
  112.8 2.0 copy.45
  114.8 2.9 copy.46
  117.7 2.3 subtract_convert_fusion.1
  120.2 1.3 copy.47
  121.5 1.3 copy.48
  122.8 2.5 pad_maximum_fusion
  125.4 5.7 %copy.49 = bf16[3,512,1024]{1,0,2:T(4,128)(2,1)} copy(bf16[3,512,1024]{2,1,0:T(8,128)(2,1)S(1)} %pad_maximum_fusion) | data formatting | bytes 6291456 | tf_op jit(solution)/shard_map/stack | solution.py:97
  131.1 5.0 %all-to-all-start = ((bf16[3,512,1024]{1,0,2:T(4,128)(2,1)}), bf16[3,512,1024]{1,0,2:T(4,128)(2,1)}, u32[]{:S(2)}, u32[]{:S(2)}) async-start(bf16[3,512,1024]{1,0,2:T(4,128)(2,1)} %copy.49), calls=%async_computation | async-start | bytes 8388608 | tf_op jit(solution)/shard_map/all_to_all | solution.py:96
  136.2 106.7 %all_gather.42 = bf16[2816,128]{1,0:T(8,128)(2,1)} all-gather(bf16[704,128]{1,0:T(8,128)(2,1)S(1)} %copy-done.4), channel_id=1, replica_groups=mesh['dp'=8,'mp'=4] {'mp'}, dimensions={0}, use_global_device_ids=true | all-gather | bytes 901120 | tf_op jit(solution)/shard_map/all_gather | solution.py:124
  242.9 11.9 %all-gather.2 = s32[4,1,512]{2,1,0:T(1,128)S(1)} all-gather(s32[1,1,512]{2,1,0:T(1,128)S(1)} %bitcast.135), channel_id=1, replica_groups=mesh['dp'=8,'mp'=4] {'mp'}, dimensions={0}, use_global_device_ids=true | all-gather | bytes 10240 | tf_op jit(solution)/shard_map/all_gather | solution.py:101
  254.9 12.1 %all-gather.1 = s32[4,1,512]{2,1,0:T(1,128)S(1)} all-gather(s32[1,1,512]{2,1,0:T(1,128)S(1)} %bitcast.136), channel_id=1, replica_groups=mesh['dp'=8,'mp'=4] {'mp'}, dimensions={0}, use_global_device_ids=true | all-gather | bytes 10240 | tf_op jit(solution)/shard_map/all_gather | solution.py:100
  267.1 3.2 copy.50
  270.2 1.2 fusion.81
  271.4 27.1 %while.10 = (s32[]{:T(128)}, bf16[4,512,4,64]{1,3,2,0:T(8,128)(2,1)}, bf16[4,512,4,64]{1,3,2,0:T(8,128)(2,1)}, s32[4,512]{1,0:T(4,128)S(1)}, bf16[4,512,4,64]{1,...) while((s32[]{:T(128)}, ...), condition=%wide.region_4.5_spmd, body=%wide.region_1.4_spmd.sunk | while | flops 416943104 | bytes 3179681 | solution.py:56
  271.4 0.2 broadcast_compare_fusion.4
  271.7 0.2 broadcast_compare_fusion.5
  271.9 2.1 fusion.100
  274.0 4.2 %fusion.101 = bf16[4,512,4,64]{1,3,2,0:T(8,128)(2,1)} fusion(bf16[4,512,4,64]{1,3,2,0:T(8,128)(2,1)} %get-tuple-element.154, s32[]{:T(128)} %get-tuple-element.153, f32[4,512]{1,0:T(4,128)S(1)} %fusion.100, bf16[4,512,4,64]{1,3,2,0:T(8,128)(2,1)} %get-tuple-element.164, f32[4]{0:T(128)S(1)} %get-tuple-element.140, f32[4]{0:T(128)S(1)} %get-tuple-element.141, ...), kind=kOutput, calls=%fused_computation.14.clone.1 | convolution fusion | flops 275909120 | bytes 1584128 | tf_op jit(solution)/shard_map/while/body/eval_jaxpr/hqk,khd->qhd/dot_general | solution.py:51
  278.2 0.2 broadcast_compare_fusion.4
  278.4 0.2 broadcast_compare_fusion.5
  278.7 2.1 fusion.100
  280.8 4.2 %fusion.101 = bf16[4,512,4,64]{1,3,2,0:T(8,128)(2,1)} fusion(bf16[4,512,4,64]{1,3,2,0:T(8,128)(2,1)} %get-tuple-element.154, s32[]{:T(128)} %get-tuple-element.153, f32[4,512]{1,0:T(4,128)S(1)} %fusion.100, bf16[4,512,4,64]{1,3,2,0:T(8,128)(2,1)} %get-tuple-element.164, f32[4]{0:T(128)S(1)} %get-tuple-element.140, f32[4]{0:T(128)S(1)} %get-tuple-element.141, ...), kind=kOutput, calls=%fused_computation.14.clone.1 | convolution fusion | flops 275909120 | bytes 1584128 | tf_op jit(solution)/shard_map/while/body/eval_jaxpr/hqk,khd->qhd/dot_general | solution.py:51
  285.0 0.2 broadcast_compare_fusion.4
  285.2 0.2 broadcast_compare_fusion.5
  285.4 2.1 fusion.100
  287.5 4.2 %fusion.101 = bf16[4,512,4,64]{1,3,2,0:T(8,128)(2,1)} fusion(bf16[4,512,4,64]{1,3,2,0:T(8,128)(2,1)} %get-tuple-element.154, s32[]{:T(128)} %get-tuple-element.153, f32[4,512]{1,0:T(4,128)S(1)} %fusion.100, bf16[4,512,4,64]{1,3,2,0:T(8,128)(2,1)} %get-tuple-element.164, f32[4]{0:T(128)S(1)} %get-tuple-element.140, f32[4]{0:T(128)S(1)} %get-tuple-element.141, ...), kind=kOutput, calls=%fused_computation.14.clone.1 | convolution fusion | flops 275909120 | bytes 1584128 | tf_op jit(solution)/shard_map/while/body/eval_jaxpr/hqk,khd->qhd/dot_general | solution.py:51
  291.8 0.2 broadcast_compare_fusion.4
  292.0 0.2 broadcast_compare_fusion.5
  292.2 2.1 fusion.100
  294.3 4.2 %fusion.101 = bf16[4,512,4,64]{1,3,2,0:T(8,128)(2,1)} fusion(bf16[4,512,4,64]{1,3,2,0:T(8,128)(2,1)} %get-tuple-element.154, s32[]{:T(128)} %get-tuple-element.153, f32[4,512]{1,0:T(4,128)S(1)} %fusion.100, bf16[4,512,4,64]{1,3,2,0:T(8,128)(2,1)} %get-tuple-element.164, f32[4]{0:T(128)S(1)} %get-tuple-element.140, f32[4]{0:T(128)S(1)} %get-tuple-element.141, ...), kind=kOutput, calls=%fused_computation.14.clone.1 | convolution fusion | flops 275909120 | bytes 1584128 | tf_op jit(solution)/shard_map/while/body/eval_jaxpr/hqk,khd->qhd/dot_general | solution.py:51
  298.5 3.7 %all-to-all-start.1 = ((bf16[4,512,256]{1,2,0:T(8,128)(2,1)}), bf16[4,512,256]{1,2,0:T(8,128)(2,1)S(1)}, u32[]{:S(2)}, u32[]{:S(2)}) async-start(bf16[4,512,256]{1,2,0:T(8,128)(2,1)} %bitcast.24), calls=%async_computation.1 | async-start | bytes 2097152 | tf_op jit(solution)/shard_map/all_to_all | solution.py:106
  302.3 2.9 copy.51
  305.2 15.7 %all-to-all-done.1 = bf16[4,512,256]{1,2,0:T(8,128)(2,1)S(1)} async-done(((bf16[4,512,256]{1,2,0:T(8,128)(2,1)}), bf16[4,512,256]{1,2,0:T(8,128)(2,1)S(1)}, u32[]{:S(2)}, u32[]{:S(2)}) %all-to-all-start.1) | async-done | bytes 1048608 | tf_op jit(solution)/shard_map/all_to_all | solution.py:106
  320.9 1.0 copy-done.3
  321.9 3.0 fusion.60
  324.9 13.2 %convolution_bitcast_fusion = f32[2,512,2816]{2,1,0:T(8,128)} fusion(bf16[2,1024,2816]{2,1,0:T(8,128)(2,1)} %all-gather.13.cloned.1.call-done, bf16[512,1024]{1,0:T(8,128)(2,1)S(1)} %get-tuple-element.84, f32[1024]{0:T(1024)S(1)} %bitcast.131, f32[512]{0:T(512)S(1)} %add_rsqrt_fusion), kind=kOutput, calls=%fused_computation.41 | convolution fusion | flops 5907677184 | bytes 24123392 | tf_op jit(solution)/shard_map/rc,jcf->jrf/dot_general | solution.py:117
  338.2 10.2 %fusion.63 = bf16[512,1024]{1,0:T(8,128)(2,1)} fusion(bf16[512,1024]{1,0:T(8,128)(2,1)S(1)} %get-tuple-element.84, bf16[2816,1024]{1,0:T(8,128)(2,1)} %all-gather.15.cloned.1.call-done, f32[2,512,2816]{2,1,0:T(8,128)} %convolution_bitcast_fusion), kind=kOutput, calls=%fused_computation.62 | convolution fusion | flops 2963013632 | bytes 19398656 | tf_op jit(solution)/shard_map/dot_general | solution.py:125
  (49 shorter events, 0.6 us)
Async XLA Ops:
  6.5 260.5 %copy-start = (f32[2,16]{1,0:T(2,128)S(1)}, f32[2,16]{1,0:T(2,128)}, u32[]{:S(2)}) copy-start(f32[2,16]{1,0:T(2,128)} %param.16) | copy-start | bytes 388
  6.5 55.1 %copy-start.8 = (s32[512]{0:T(512)S(1)}, s32[512]{0:T(512)}, u32[]{:S(2)}) copy-start(s32[512]{0:T(512)} %param.21) | copy-start | bytes 6148
  6.5 55.2 %copy-start.2 = (bf16[512,1024]{1,0:T(8,128)(2,1)S(1)}, bf16[512,1024]{1,0:T(8,128)(2,1)}, u32[]{:S(2)}) copy-start(bf16[512,1024]{1,0:T(8,128)(2,1)} %param.12) | copy-start | bytes 3145732
  6.5 50.2 %all-gather.11.cloned.1.call-start = ((), (), s32[]{:S(2)}) async-start(), calls=%async_computation.3 | async-start | bytes 1802240 | tf_op jit(solution)/shard_map/all_gather | solution.py:115
  8.7 53.3 %copy-start.5 = (f32[2,1024]{1,0:T(2,128)S(1)}, f32[2,1024]{1,0:T(2,128)}, u32[]{:S(2)}) copy-start(f32[2,1024]{1,0:T(2,128)} %param.13) | copy-start | bytes 24580
  8.8 94.8 %all-gather.9.cloned.1.call-start = ((), (), s32[]{:S(2)}) async-start(), calls=%async_computation.2 | async-start | bytes 7077888 | tf_op jit(solution)/shard_map/all_gather | solution.py:90
  36.5 265.8 %all-gather.17.cloned.1.call-start = ((), (), s32[]{:S(2)}) async-start(), calls=%async_computation.6 | async-start | bytes 2359296 | tf_op jit(solution)/shard_map/all_gather | solution.py:110
  55.5 269.4 %all-gather.13.cloned.1.call-start = ((), (), s32[]{:S(2)}) async-start(), calls=%async_computation.4 | async-start | bytes 12976128 | tf_op jit(solution)/shard_map/all_gather | solution.py:120
  131.1 5.1 %copy-start.4 = (bf16[704,128]{1,0:T(8,128)(2,1)S(1)}, bf16[704,128]{1,0:T(8,128)(2,1)}, u32[]{:S(2)}) copy-start(bf16[704,128]{1,0:T(8,128)(2,1)} %param.18) | copy-start | bytes 540676
  131.1 111.8 %copy-start.6 = (s32[512]{0:T(512)S(1)}, s32[512]{0:T(512)}, u32[]{:S(2)}) copy-start(s32[512]{0:T(512)} %param.20) | copy-start | bytes 6148
  131.1 123.8 %copy-start.7 = (s32[512]{0:T(512)S(1)}, s32[512]{0:T(512)}, u32[]{:S(2)}) copy-start(s32[512]{0:T(512)} %param.19) | copy-start | bytes 6148
  131.1 136.0 %all-to-all-start = ((bf16[3,512,1024]{1,0,2:T(4,128)(2,1)}), bf16[3,512,1024]{1,0,2:T(4,128)(2,1)}, u32[]{:S(2)}, u32[]{:S(2)}) async-start(bf16[3,512,1024]{1,0,2:T(4,128)(2,1)} %copy.49), calls=%async_computation | async-start | bytes 8388608 | tf_op jit(solution)/shard_map/all_to_all | solution.py:96
  136.1 202.1 %all-gather.15.cloned.1.call-start = ((), (), s32[]{:S(2)}) async-start(), calls=%async_computation.5 | async-start | bytes 6488064 | tf_op jit(solution)/shard_map/all_gather | solution.py:127
  298.5 22.4 %all-to-all-start.1 = ((bf16[4,512,256]{1,2,0:T(8,128)(2,1)}), bf16[4,512,256]{1,2,0:T(8,128)(2,1)S(1)}, u32[]{:S(2)}, u32[]{:S(2)}) async-start(bf16[4,512,256]{1,2,0:T(8,128)(2,1)} %bitcast.24), calls=%async_computation.1 | async-start | bytes 2097152 | tf_op jit(solution)/shard_map/all_to_all | solution.py:106
  320.9 1.0 copy-start.3
  338.2 10.2 %copy-start.1 = (f32[2,16]{1,0:T(2,128)S(1)}, f32[2,16]{1,0:T(2,128)}, u32[]{:S(2)}) copy-start(f32[2,16]{1,0:T(2,128)} %param.16) | copy-start | bytes 388
Sparse Core Ops, SparseCore 0:
  8.9 47.8 all-gather.10
  58.7 44.7 all-gather.8
  105.4 27.7 all-gather.16
  135.0 67.5 all-gather.12
  243.0 44.1 all-gather.14
